TPU v7x, 512 devices: a 4x2x32 block of a 4x16x32 slice. The times are simulated.
512 devices in a mesh: parts: 2 (over y), row: 32 (over z), col: 4 (over x), sub: 2 (over core).
Axes of the slice: x: 4, y: 2, z: 32, core: 2. Of those that a mesh axis runs over, the one named last changes fastest.
The devices are a block of a 4x16x32 slice.
Arguments:
- pair: float32 [768, 384, 128], P(('parts', 'row'), ('col', 'sub')), parts along dimension 0, may hold values from -250 to 250, as said below
- residue_mask: int32 [768], P('parts'), parts along dimension 0, may hold values from 0 to 1, as said below
- tri_norm_gain: float32 [128], replicated, may hold values from 0.25 to 1.75
- tri_in_weight: bfloat16 [128, 4, 128], replicated, may hold values from -0.5 to 0.5
- tri_gate_weight: bfloat16 [128, 128], replicated, may hold values from -0.5 to 0.5
- tri_out_norm_gain: float32 [128], replicated, may hold values from 0.25 to 1.75
- tri_out_weight: bfloat16 [128, 128], replicated, may hold values from -0.5 to 0.5
- att_norm_gain: float32 [128], replicated, may hold values from 0.25 to 1.75
- att_proj_weight: bfloat16 [128, 4, 128], replicated, may hold values from -0.5 to 0.5
- att_bias_weight: bfloat16 [128, 4], replicated, may hold values from -15 to 15
- att_out_weight: bfloat16 [128, 128], replicated, may hold values from -0.5 to 0.5
Outputs:
- pair_out: float32 [768, 384, 128], P(('parts', 'row'), ('col', 'sub')), parts along dimension 0
There are 2 independent parts, one for each index of `parts`. A program takes and returns all parts, laid end to end along the dimension named above; an argument that names none is the same for every part. Nothing has to cross between parts.
Inputs may be any that keep to these rules, and one draw needn't show every extreme that they name: The pair entries are finite. `residue_mask`: 0 on every residue at or above a length of at least 192 and less than 384; below it 1, except some unresolved residues that are 0; residue 0 is always 1.
All inputs are finite; a program needn't handle non-finite values.
Results may differ from a plain program's by a relative error of at most 0.0032.
Values may be sent and summed in bfloat16 or wider, within the bound.
A program may use at most 64 MiB of HBM per device.

v0:
```python
import math
import jax
import jax.numpy as jnp
from jax import lax
from jax.sharding import PartitionSpec as P

epsilon = 1e-05
mask_penalty = 1000000000.0


def split_up(array, dim, devices):
    lengths = array.shape
    pieces = array.reshape(*lengths[:dim], devices, lengths[dim] // devices, *lengths[dim + 1 :])
    return jnp.moveaxis(pieces, dim, 0)


def sum_at_owner(array, axis, dim):
    devices = lax.axis_size(axis)
    pieces = lax.all_to_all(split_up(array, dim, devices), axis, 0, 0, tiled=True)
    return jnp.sum(pieces, axis=0)


def in_one_piece(arrays, axis, dim, along):
    widths = [a.shape[along] for a in arrays]
    both = jnp.concatenate(arrays, axis=along)
    result = lax.all_gather(both, axis, axis=dim, tiled=True)
    return tuple(jnp.split(result, [sum(widths[:k]) for k in range(1, len(widths))], axis=along))


def from_everyone(array, axis):
    copies = jnp.broadcast_to(array, (lax.axis_size(axis), *array.shape))
    return lax.all_to_all(copies, axis, split_axis=0, concat_axis=0, tiled=True)


def laid_out(pieces, dim):
    lengths = list(pieces.shape[1:])
    lengths[dim] *= pieces.shape[0]
    return jnp.moveaxis(pieces, 0, dim).reshape(lengths)


def gathered_copies(array, axis, dim):
    pieces = from_everyone(array, axis)
    return laid_out(pieces, dim)


def norm_last(values_in, gain):
    center = jnp.mean(values_in, axis=-1, keepdims=True)
    centered = values_in - center
    variance = jnp.mean(centered * centered, axis=-1, keepdims=True)
    return centered * lax.rsqrt(variance + epsilon) * gain


def project(normed, weight):
    flat_rows = normed.reshape(-1, normed.shape[-1])
    product = jnp.dot(flat_rows, weight, preferred_element_type=jnp.float32)
    return product.reshape(normed.shape[:-1] + (weight.shape[1],))


def body(
    pair,
    residue_mask,
    tri_norm_gain,
    tri_in_weight,
    tri_gate_weight,
    tri_out_norm_gain,
    tri_out_weight,
    att_norm_gain,
    att_proj_weight,
    att_bias_weight,
    att_out_weight,
):
    rows_here, cols_here, chan_here = pair.shape
    residues = cols_here * lax.axis_size(("col", "sub"))
    row_offset = lax.axis_index("row") * rows_here
    col_offset = lax.axis_index(("col", "sub")) * cols_here
    residue_live = residue_mask.astype(jnp.float32)
    live_rows = lax.dynamic_slice_in_dim(residue_live, row_offset, rows_here)
    live_cols = lax.dynamic_slice_in_dim(residue_live, col_offset, cols_here)
    pair_live = (live_rows[:, None] * live_cols[None, :])[:, :, None]
    tri_normed = norm_last(pair, tri_norm_gain).astype(jnp.bfloat16)
    in_width = tri_in_weight.shape[2]
    projected = project(tri_normed, tri_in_weight.reshape(tri_in_weight.shape[0], -1)).reshape(
        rows_here, cols_here, 4, in_width
    )
    left_factor = (jax.nn.sigmoid(projected[:, :, 0]) * projected[:, :, 1] * pair_live).astype(
        jnp.bfloat16
    )
    right_factor = (jax.nn.sigmoid(projected[:, :, 2]) * projected[:, :, 3] * pair_live).astype(
        jnp.bfloat16
    )
    terms = jnp.einsum(
        "ikh,jkh->ijh",
        left_factor,
        lax.all_gather(right_factor, "row", axis=0, tiled=True),
        preferred_element_type=jnp.float32,
    )
    tri_sum = sum_at_owner(terms, ("col", "sub"), 1)
    hidden_normed = norm_last(tri_sum, tri_out_norm_gain).astype(jnp.bfloat16)
    tri_gate = jax.nn.sigmoid(project(tri_normed, tri_gate_weight))
    pair_mid = pair + tri_gate * project(hidden_normed, tri_out_weight)
    att_normed = norm_last(pair_mid, att_norm_gain).astype(jnp.bfloat16)
    head_width = att_proj_weight.shape[2]
    heads_here = att_bias_weight.shape[1]
    head_size = head_width // heads_here
    projected = project(att_normed, att_proj_weight.reshape(att_proj_weight.shape[0], -1)).reshape(
        rows_here, cols_here, 4, head_width
    )
    queries = (projected[:, :, 0] * head_size ** (-0.5)).astype(jnp.bfloat16)
    key_rows = projected[:, :, 1].astype(jnp.bfloat16)
    value_rows = projected[:, :, 2].astype(jnp.bfloat16)
    att_gate = jax.nn.sigmoid(projected[:, :, 3])
    pair_bias = project(att_normed, att_bias_weight).astype(jnp.bfloat16)
    key_all, value_all = in_one_piece((key_rows, value_rows), ("col", "sub"), 1, 0)
    bias_all_rows = gathered_copies(pair_bias, "row", 0)
    bias_panel = lax.all_to_all(
        bias_all_rows, ("col", "sub"), split_axis=0, concat_axis=1, tiled=True
    )
    mask_row = (residue_live - 1.0) * mask_penalty
    head_bias = jnp.transpose(bias_panel.astype(jnp.float32), (2, 0, 1)) + mask_row[None, None, :]
    block_rows = math.gcd(rows_here, max(1, 512 // cols_here))
    blocks = rows_here // block_rows

    def attend(block_items):
        query_block, key_block, value_block = block_items
        scores = (
            jnp.einsum(
                "ijhd,ikhd->ihjk", query_block, key_block, preferred_element_type=jnp.float32
            )
            + head_bias[None]
        )
        row_max = jnp.max(scores, axis=-1, keepdims=True)
        raised = jnp.exp(scores - row_max)
        weights = (raised / jnp.sum(raised, axis=-1, keepdims=True)).astype(jnp.bfloat16)
        return jnp.einsum(
            "ihjk,ikhd->ijhd", weights, value_block, preferred_element_type=jnp.float32
        )

    attended = lax.map(
        attend,
        (
            queries.reshape(blocks, block_rows, cols_here, heads_here, head_size),
            key_all.reshape(blocks, block_rows, residues, heads_here, head_size),
            value_all.reshape(blocks, block_rows, residues, heads_here, head_size),
        ),
    )
    gated = (attended.reshape(rows_here, cols_here, head_width) * att_gate).astype(jnp.bfloat16)
    return pair_mid + project(gated, att_out_weight)


def solution(mesh):
    placed = (
        P(("parts", "row"), ("col", "sub"), None),
        P("parts"),
        P(),
        P(),
        P(),
        P(),
        P(),
        P(),
        P(),
        P(),
        P(),
    )
    return jax.shard_map(
        body,
        mesh=mesh,
        in_specs=placed,
        out_specs=P(("parts", "row"), ("col", "sub"), None),
        check_vma=False,
    )
```

profile of v0, /device:TPU:33, one launch (start us, length us, event | category | flops | bytes accessed | tf_op | source)
XLA Modules:
  0.0 341.0 jit_solution(17317028375399813214)
XLA Ops:
  6.6 0.7 convert_element_type.59
  7.5 1.1 reduce_sum.72
  8.6 1.2 multiply_reduce_fusion.2
  9.8 0.9 copy.126
  11.0 0.4 fusion.51
  11.3 0.8 fusion.33
  12.3 1.2 copy.102
  13.5 147.5 %all-gather.3.cloned.1.call-done = bf16[384,48,128]{2,1,0:T(8,128)(2,1)} async-done(((bf16[12,48,128]{2,1,0:T(8,128)(2,1)}), bf16[384,48,128]{2,1,0:T(8,128)(2,1)}) %all-gather.3.cloned.1.call-update) | async-done | bytes 4718608 | tf_op jit(solution)/shard_map/all_gather | solution.py:94
  160.9 17.8 %copy.101 = bf16[384,48,128]{1,0,2:T(8,128)(2,1)} copy(bf16[384,48,128]{2,1,0:T(8,128)(2,1)} %all-gather.3.cloned.1.call-done) | data formatting | bytes 9437184 | tf_op jit(solution)/shard_map/all_gather | solution.py:94
  178.7 9.1 %convolution_bitcast_fusion.1 = f32[12,384,128]{1,0,2:T(8,128)S(1)} fusion(bf16[384,48,128]{1,0,2:T(8,128)(2,1)} %copy.101, bf16[12,48,128]{1,0,2:T(8,128)(2,1)} %copy.102), kind=kOutput, calls=%fused_computation.18 | convolution fusion | flops 56623104 | bytes 7225344 | tf_op jit(solution)/shard_map/ikh,jkh->ijh/dot_general | solution.py:91
  187.8 2.1 copy.103
  190.0 3.3 copy.104
  193.2 23.9 %all-to-all-start = ((f32[8,12,48,128]{3,2,1,0:T(8,128)}), f32[8,12,48,128]{3,2,1,0:T(8,128)S(1)}, u32[]{:S(2)}, u32[]{:S(2)}) async-start(f32[8,12,48,128]{3,2,1,0:T(8,128)} %copy.104), calls=%async_computation | async-start | bytes 4718592 | tf_op jit(solution)/shard_map/all_to_all | solution.py:19
  217.4 0.3 fusion.23
  217.7 28.5 %all-to-all-done = f32[8,12,48,128]{3,2,1,0:T(8,128)S(1)} async-done(((f32[8,12,48,128]{3,2,1,0:T(8,128)}), f32[8,12,48,128]{3,2,1,0:T(8,128)S(1)}, u32[]{:S(2)}, u32[]{:S(2)}) %all-to-all-start) | async-done | bytes 2359328 | tf_op jit(solution)/shard_map/all_to_all | solution.py:19
  246.7 0.4 fusion.69
  247.5 0.4 fusion.70
  247.9 0.7 pad_maximum_fusion
  248.8 0.3 convolution_convert_fusion
  249.2 1.2 reshape.185
  250.4 12.5 %all-to-all-start.1 = ((bf16[32,2,1152]{2,1,0:T(2,128)(2,1)}), bf16[32,2,1152]{2,1,0:T(2,128)(2,1)S(1)}, u32[]{:S(2)}, u32[]{:S(2)}) async-start(bf16[32,2,1152]{2,1,0:T(2,128)(2,1)} %reshape.185), calls=%async_computation.1 | async-start | bytes 294912 | tf_op jit(solution)/shard_map/all_to_all | solution.py:32
  263.0 30.6 %all-to-all-done.1 = bf16[32,2,1152]{2,1,0:T(2,128)(2,1)S(1)} async-done(((bf16[32,2,1152]{2,1,0:T(2,128)(2,1)}), bf16[32,2,1152]{2,1,0:T(2,128)(2,1)S(1)}, u32[]{:S(2)}, u32[]{:S(2)}) %all-to-all-start.1) | async-done | bytes 147488 | tf_op jit(solution)/shard_map/all_to_all | solution.py:32
  293.5 0.4 reshape.186
  293.9 1.2 reshape.187
  295.1 5.9 %all-to-all-start.2 = ((bf16[8,2,4608]{2,1,0:T(2,128)(2,1)}), bf16[8,2,4608]{2,1,0:T(2,128)(2,1)S(1)}, u32[]{:S(2)}, u32[]{:S(2)}) async-start(bf16[8,2,4608]{2,1,0:T(2,128)(2,1)} %reshape.187), calls=%async_computation.2 | async-start | bytes 294912 | tf_op jit(solution)/shard_map/all_to_all | solution.py:115
  301.3 5.2 %all-to-all-done.2 = bf16[8,2,4608]{2,1,0:T(2,128)(2,1)S(1)} async-done(((bf16[8,2,4608]{2,1,0:T(2,128)(2,1)}), bf16[8,2,4608]{2,1,0:T(2,128)(2,1)S(1)}, u32[]{:S(2)}, u32[]{:S(2)}) %all-to-all-start.2) | async-done | bytes 147488 | tf_op jit(solution)/shard_map/all_to_all | solution.py:115
  306.5 0.4 reshape.188
  307.1 0.3 reshape.176
  307.4 0.4 copy.111
  308.1 1.8 fusion.68
  309.9 1.4 copy.107
  311.3 0.7 copy.109
  312.1 18.8 %while.10 = (s32[]{:T(128)}, f32[6,2,48,4,32]{2,4,3,1,0:T(8,128)}, bf16[6,2,384,4,32]{2,4,3,1,0:T(8,128)(2,1)}, bf16[6,2,48,4,32]{2,4,3,1,0:T(8,128)(2,1)S(1)}, ...) while((s32[]{:T(128)}, f32[6,2,48,4,32]{2,4,3,1,0:T(8,128)}, ...), condition=%wide.region_10.11_spmd, body=%wide.region_7.10_spmd.sunk | while | flops 29344896 | bytes 3220045 | solution.py:138
  312.1 0.3 convolution_add_fusion.3
  312.4 0.5 fusion.90
  312.8 2.4 fusion.91
  315.5 0.5 fusion.90
  316.0 2.4 fusion.91
  318.7 0.5 fusion.90
  319.1 2.4 fusion.91
  321.8 0.5 fusion.90
  322.2 2.4 fusion.91
  324.9 0.5 fusion.90
  325.4 2.4 fusion.91
  328.1 0.5 fusion.90
  328.5 2.4 fusion.91
  330.9 1.4 copy.113
  332.3 1.9 convolution_add_fusion.1
  (56 shorter events, 3.8 us)
Async XLA Ops:
  6.5 240.2 %copy-start = (bf16[128,128]{1,0:T(8,128)(2,1)S(1)}, bf16[128,128]{1,0:T(8,128)(2,1)}, u32[]{:S(2)}) copy-start(bf16[128,128]{1,0:T(8,128)(2,1)} %param.19) | copy-start | bytes 98308
  6.6 4.4 %copy-start.1 = (f32[12,48,128]{2,1,0:T(8,128)S(1)}, f32[12,48,128]{2,1,0:T(8,128)}, u32[]{:S(2)}) copy-start(f32[12,48,128]{2,1,0:T(8,128)} %param.13) | copy-start | bytes 884740
  6.6 4.4 %copy-start.7 = (f32[128]{0:T(128)S(1)}, f32[128]{0:T(128)}, u32[]{:S(2)}) copy-start(f32[128]{0:T(128)} %param.15) | copy-start | bytes 1540
  6.6 154.4 %all-gather.3.cloned.1.call-start = ((), (), s32[]{:S(2)}) async-start(), calls=%async_computation.3 | async-start | bytes 4866048 | tf_op jit(solution)/shard_map/all_gather | solution.py:94
  193.2 24.0 %copy-start.3 = (bf16[128,4,128]{2,1,0:T(4,128)(2,1)S(1)}, bf16[128,4,128]{2,1,0:T(4,128)(2,1)}, u32[]{:S(2)}) copy-start(bf16[128,4,128]{2,1,0:T(4,128)(2,1)} %param.21) | copy-start | bytes 393220
  193.2 24.1 %copy-start.9 = (bf16[128,128]{1,0:T(8,128)(2,1)S(1)}, bf16[128,128]{1,0:T(8,128)(2,1)}, u32[]{:S(2)}) copy-start(bf16[128,128]{1,0:T(8,128)(2,1)} %param.17) | copy-start | bytes 98308
  193.2 53.0 %all-to-all-start = ((f32[8,12,48,128]{3,2,1,0:T(8,128)}), f32[8,12,48,128]{3,2,1,0:T(8,128)S(1)}, u32[]{:S(2)}, u32[]{:S(2)}) async-start(f32[8,12,48,128]{3,2,1,0:T(8,128)} %copy.104), calls=%async_computation | async-start | bytes 4718592 | tf_op jit(solution)/shard_map/all_to_all | solution.py:19
  217.2 90.9 %all-gather.5.cloned.1.call-start = ((), (), s32[]{:S(2)}) async-start(), calls=%async_computation.4 | async-start | bytes 2654208 | tf_op jit(solution)/shard_map/all_gather | solution.py:26
  217.7 29.0 %copy-start.8 = (f32[128]{0:T(128)S(1)}, f32[128]{0:T(128)}, u32[]{:S(2)}) copy-start(f32[128]{0:T(128)} %param.18) | copy-start | bytes 1540
  246.4 1.1 copy-start.5
  247.9 53.2 %copy-start.2 = (f32[12,48,4,128]{3,1,2,0:T(8,128)}, f32[12,48,4,128]{3,1,2,0:T(8,128)S(1)}, u32[]{:S(2)}) copy-start(f32[12,48,4,128]{3,1,2,0:T(8,128)S(1)} %get-tuple-element.67) | copy-start | bytes 3538948
  247.9 0.9 copy-start.6
  247.9 15.0 %copy-start.4 = (s32[384]{0:T(512)S(1)}, s32[384]{0:T(512)}, u32[]{:S(2)}) copy-start(s32[384]{0:T(512)} %param.14) | copy-start | bytes 4612
  250.4 43.1 %all-to-all-start.1 = ((bf16[32,2,1152]{2,1,0:T(2,128)(2,1)}), bf16[32,2,1152]{2,1,0:T(2,128)(2,1)S(1)}, u32[]{:S(2)}, u32[]{:S(2)}) async-start(bf16[32,2,1152]{2,1,0:T(2,128)(2,1)} %reshape.185), calls=%async_computation.1 | async-start | bytes 294912 | tf_op jit(solution)/shard_map/all_to_all | solution.py:32
  295.1 11.4 %all-to-all-start.2 = ((bf16[8,2,4608]{2,1,0:T(2,128)(2,1)}), bf16[8,2,4608]{2,1,0:T(2,128)(2,1)S(1)}, u32[]{:S(2)}, u32[]{:S(2)}) async-start(bf16[8,2,4608]{2,1,0:T(2,128)(2,1)} %reshape.187), calls=%async_computation.2 | async-start | bytes 294912 | tf_op jit(solution)/shard_map/all_to_all | solution.py:115
  312.0 20.2 %copy-start.10 = (bf16[128,128]{1,0:T(8,128)(2,1)S(1)}, bf16[128,128]{1,0:T(8,128)(2,1)}, u32[]{:S(2)}) copy-start(bf16[128,128]{1,0:T(8,128)(2,1)} %param.23) | copy-start | bytes 98308
Sparse Core Ops, SparseCore 0:
  12.4 148.5 all-gather.2
  248.9 31.5 all-gather.4
where the time goes:
time: 342 us; the launch traced here: 341 us
  waiting for transfers between devices  212 us (62%)
  starting transfers between devices  42.3 us (12%)
  local copies, waits for them, and re-layouts  35.8 us (10%)
  matrix products  31.6 us (9%)
  between operations  13.8 us (4%)
  other arithmetic  5.57 us (2%)
    all_gather x1, waiting for transfers between devices, body(): lax.all_gather(right_factor, 'row', axis=0, tiled=True)  147 us
    all_to_all x1, waiting for transfers between devices, from_everyone(): return lax.all_to_all(copies, axis, split_axis=0, concat_axis=0, tiled=True)  30.6 us
    all_to_all x1, waiting for transfers between devices, sum_at_owner(): lax.all_to_all(split_up(array, dim, devices), axis, 0, 0, tiled=True)  28.5 us
    all_to_all x1, starting transfers between devices, sum_at_owner(): lax.all_to_all(split_up(array, dim, devices), axis, 0, 0, tiled=True)  23.9 us
    all_gather x1, local copies, waits for them, and re-layouts, body(): lax.all_gather(right_factor, 'row', axis=0, tiled=True)  17.8 us
    dot_general x6, matrix products, attend(): jnp.einsum('ihjk,ikhd->ijhd', weights, value_block, preferred_element_typ...  14.3 us
    all_to_all x1, starting transfers between devices, from_everyone(): return lax.all_to_all(copies, axis, split_axis=0, concat_axis=0, tiled=True)  12.5 us
    dot_general x1, matrix products, body(): jnp.einsum('ikh,jkh->ijh', left_factor, lax.all_gather(right_factor, 'row...  9.08 us
  transfers between devices with their start and end apart: 5, of which 4 were waited for; matrix products, arithmetic and copies ran while one was open for 2% of the time, Pallas kernels for 0%

commit v1 on v0

--- a/solution.py
+++ b/solution.py
@@ -91,7 +91,9 @@
     terms = jnp.einsum(
         "ikh,jkh->ijh",
         left_factor,
-        lax.all_gather(right_factor, "row", axis=0, tiled=True),
+        jnp.concatenate(
+            lax.all_to_all(jnp.stack([right_factor] * lax.axis_size("row")), "row", 0, 0), axis=0
+        ),
         preferred_element_type=jnp.float32,
     )
     tri_sum = sum_at_owner(terms, ("col", "sub"), 1)

time: 342 us -> 637 us (1.86)
  waiting for transfers between devices: 212 us -> 469 us
  starting transfers between devices: 42.3 us -> 78.9 us
    all_to_all x0 -> x1, waiting for transfers between devices: none -> 405 us  [body(): lax.all_to_all(jnp.stack([right_factor] * lax.axis_size('row')), 'row', 0...]
    all_gather x1 -> x0, waiting for transfers between devices: 147 us -> none  [body(): lax.all_gather(right_factor, 'row', axis=0, tiled=True)]
    all_to_all x0 -> x1, starting transfers between devices: none -> 46.3 us  [body(): lax.all_to_all(jnp.stack([right_factor] * lax.axis_size('row')), 'row', 0...]
    all_to_all x1, starting transfers between devices: 23.9 us -> 5.57 us  [sum_at_owner(): lax.all_to_all(split_up(array, dim, devices), axis, 0, 0, tiled=True)]
    all_gather x1 -> x0, local copies, waits for them, and re-layouts: 17.8 us -> none  [body(): lax.all_gather(right_factor, 'row', axis=0, tiled=True)]
    all_to_all x1, starting transfers between devices: 12.5 us -> 21.1 us  [from_everyone(): return lax.all_to_all(copies, axis, split_axis=0, concat_axis=0, tiled=True)]
    reshape x0 -> x1, local copies, waits for them, and re-layouts: none -> 7.59 us  [body(): jnp.concatenate(lax.all_to_all(jnp.stack([right_factor] * lax.axis_size('...]
  transfers between devices with their start and end apart: 5 -> 5, of which waited for: 4 -> 4; matrix products, arithmetic and copies ran while one was open for 2% -> 1% of each run, Pallas kernels for 0% -> 0%
where the time goes in v1:
time: 637 us; the launch traced here: 635 us
  waiting for transfers between devices  469 us (74%)
  starting transfers between devices  78.9 us (12%)
  matrix products  37 us (6%)
  local copies, waits for them, and re-layouts  31.5 us (5%)
  between operations  13.8 us (2%)
    all_to_all x1, waiting for transfers between devices, body(): lax.all_to_all(jnp.stack([right_factor] * lax.axis_size('row')), 'row', 0...  405 us
    all_to_all x1, starting transfers between devices, body(): lax.all_to_all(jnp.stack([right_factor] * lax.axis_size('row')), 'row', 0...  46.3 us
    all_to_all x1, waiting for transfers between devices, from_everyone(): return lax.all_to_all(copies, axis, split_axis=0, concat_axis=0, tiled=True)  30.6 us
    all_to_all x1, waiting for transfers between devices, sum_at_owner(): lax.all_to_all(split_up(array, dim, devices), axis, 0, 0, tiled=True)  28.5 us
    all_to_all x1, starting transfers between devices, from_everyone(): return lax.all_to_all(copies, axis, split_axis=0, concat_axis=0, tiled=True)  21.1 us
    dot_general x6, matrix products, attend(): jnp.einsum('ihjk,ikhd->ijhd', weights, value_block, preferred_element_typ...  14.3 us
  transfers between devices with their start and end apart: 5, of which 4 were waited for; matrix products, arithmetic and copies ran while one was open for 1% of the time, Pallas kernels for 0%

profile of v1, /device:TPU:33, one launch (start us, length us, event | category | flops | bytes accessed | tf_op | source)
XLA Modules:
  0.0 635.4 jit_solution(18206508943255735724)
XLA Ops:
  6.6 0.7 convert_element_type.61
  7.4 1.1 reduce_sum.72
  8.6 1.2 multiply_reduce_fusion.2
  9.8 0.9 copy.126
  10.9 0.4 fusion.51
  11.5 3.2 stack.2
  14.8 46.3 %all-to-all-start = ((bf16[32,12,48,128]{3,2,1,0:T(8,128)(2,1)}), bf16[32,12,48,128]{3,2,1,0:T(8,128)(2,1)}, u32[]{:S(2)}, u32[]{:S(2)}) async-start(bf16[32,12,48,128]{3,2,1,0:T(8,128)(2,1)} %stack.2), calls=%async_computation | async-start | bytes 9437184 | tf_op jit(solution)/shard_map/all_to_all | solution.py:95
  61.1 1.2 copy.102
  62.3 405.0 %all-to-all-done = bf16[32,12,48,128]{3,2,1,0:T(8,128)(2,1)} async-done(((bf16[32,12,48,128]{3,2,1,0:T(8,128)(2,1)}), bf16[32,12,48,128]{3,2,1,0:T(8,128)(2,1)}, u32[]{:S(2)}, u32[]{:S(2)}) %all-to-all-start) | async-done | bytes 4718624 | tf_op jit(solution)/shard_map/all_to_all | solution.py:95
  467.2 7.6 %copy.101 = bf16[384,48,128]{0,1,2:T(8,128)(2,1)} copy(bf16[384,48,128]{2,1,0:T(8,128)(2,1)} %bitcast.12) | data formatting | bytes 9437184 | tf_op jit(solution)/shard_map/reshape | solution.py:94
  474.8 3.4 convolution_bitcast_fusion.1
  478.2 2.1 copy.103
  480.4 3.3 copy.104
  483.6 5.6 all-to-all-start.1
  489.7 28.5 %all-to-all-done.1 = f32[8,12,48,128]{3,2,1,0:T(8,128)S(1)} async-done(((f32[8,12,48,128]{3,2,1,0:T(8,128)}), f32[8,12,48,128]{3,2,1,0:T(8,128)S(1)}, u32[]{:S(2)}, u32[]{:S(2)}) %all-to-all-start.1) | async-done | bytes 2359328 | tf_op jit(solution)/shard_map/all_to_all | solution.py:19
  518.7 0.4 fusion.69
  519.5 0.4 fusion.70
  519.9 0.7 pad_maximum_fusion
  521.2 1.2 reshape.194
  522.5 21.1 %all-to-all-start.2 = ((bf16[32,2,1152]{2,1,0:T(2,128)(2,1)}), bf16[32,2,1152]{2,1,0:T(2,128)(2,1)S(1)}, u32[]{:S(2)}, u32[]{:S(2)}) async-start(bf16[32,2,1152]{2,1,0:T(2,128)(2,1)} %reshape.194), calls=%async_computation.2 | async-start | bytes 294912 | tf_op jit(solution)/shard_map/all_to_all | solution.py:32
  543.6 30.6 %all-to-all-done.2 = bf16[32,2,1152]{2,1,0:T(2,128)(2,1)S(1)} async-done(((bf16[32,2,1152]{2,1,0:T(2,128)(2,1)}), bf16[32,2,1152]{2,1,0:T(2,128)(2,1)S(1)}, u32[]{:S(2)}, u32[]{:S(2)}) %all-to-all-start.2) | async-done | bytes 147488 | tf_op jit(solution)/shard_map/all_to_all | solution.py:32
  574.5 1.2 reshape.196
  575.8 5.9 all-to-all-start.3
  581.9 5.2 all-to-all-done.3
  588.7 2.8 fusion.68
  591.6 2.4 copy.107
  593.9 1.4 copy.109
  595.3 30.0 %while.10 = (s32[]{:T(128)}, f32[6,2,48,4,32]{2,4,3,1,0:T(8,128)}, bf16[6,2,384,4,32]{2,4,3,1,0:T(8,128)(2,1)}, bf16[6,2,48,4,32]{2,4,3,1,0:T(8,128)(2,1)S(1)}, ...) while((s32[]{:T(128)}, f32[6,2,48,4,32]{2,4,3,1,0:T(8,128)}, ...), condition=%wide.region_10.11_spmd, body=%wide.region_7.10_spmd.sunk | while | flops 29344896 | bytes 3220045 | solution.py:140
  595.3 1.2 convolution_add_fusion.3
  596.6 1.4 fusion.90
  597.9 2.4 fusion.91
  600.3 1.2 convolution_add_fusion.3
  601.6 1.4 fusion.90
  602.9 2.4 fusion.91
  605.3 1.2 convolution_add_fusion.3
  606.5 1.4 fusion.90
  607.9 2.4 fusion.91
  610.3 1.2 convolution_add_fusion.3
  611.5 1.4 fusion.90
  612.9 2.4 fusion.91
  615.3 1.2 convolution_add_fusion.3
  616.5 1.4 fusion.90
  617.9 2.4 fusion.91
  620.3 1.2 convolution_add_fusion.3
  621.5 1.4 fusion.90
  622.9 2.4 fusion.91
  625.3 1.4 copy.113
  626.7 1.9 convolution_add_fusion.1
  (56 shorter events, 4.6 us)
Async XLA Ops:
  6.5 512.2 %copy-start = (bf16[128,128]{1,0:T(8,128)(2,1)S(1)}, bf16[128,128]{1,0:T(8,128)(2,1)}, u32[]{:S(2)}) copy-start(bf16[128,128]{1,0:T(8,128)(2,1)} %param.19) | copy-start | bytes 98308
  6.6 4.4 copy-start.1
  6.6 4.4 copy-start.7
  14.8 452.5 %all-to-all-start = ((bf16[32,12,48,128]{3,2,1,0:T(8,128)(2,1)}), bf16[32,12,48,128]{3,2,1,0:T(8,128)(2,1)}, u32[]{:S(2)}, u32[]{:S(2)}) async-start(bf16[32,12,48,128]{3,2,1,0:T(8,128)(2,1)} %stack.2), calls=%async_computation | async-start | bytes 9437184 | tf_op jit(solution)/shard_map/all_to_all | solution.py:95
  483.6 5.6 copy-start.3
  483.6 5.7 copy-start.9
  483.6 34.6 %all-to-all-start.1 = ((f32[8,12,48,128]{3,2,1,0:T(8,128)}), f32[8,12,48,128]{3,2,1,0:T(8,128)S(1)}, u32[]{:S(2)}, u32[]{:S(2)}) async-start(f32[8,12,48,128]{3,2,1,0:T(8,128)} %copy.104), calls=%async_computation.1 | async-start | bytes 4718592 | tf_op jit(solution)/shard_map/all_to_all | solution.py:19
  489.2 99.5 %all-gather.2.cloned.1.call-start = ((), (), s32[]{:S(2)}) async-start(), calls=%async_computation.4 | async-start | bytes 2654208 | tf_op jit(solution)/shard_map/all_gather | solution.py:26
  489.7 29.0 %copy-start.8 = (f32[128]{0:T(128)S(1)}, f32[128]{0:T(128)}, u32[]{:S(2)}) copy-start(f32[128]{0:T(128)} %param.18) | copy-start | bytes 1540
  518.4 1.1 copy-start.5
  519.9 61.8 %copy-start.2 = (f32[12,48,4,128]{3,1,2,0:T(8,128)}, f32[12,48,4,128]{3,1,2,0:T(8,128)S(1)}, u32[]{:S(2)}) copy-start(f32[12,48,4,128]{3,1,2,0:T(8,128)S(1)} %get-tuple-element.67) | copy-start | bytes 3538948
  519.9 0.9 copy-start.6
  519.9 23.6 %copy-start.4 = (s32[384]{0:T(512)S(1)}, s32[384]{0:T(512)}, u32[]{:S(2)}) copy-start(s32[384]{0:T(512)} %param.14) | copy-start | bytes 4612
  522.5 51.7 %all-to-all-start.2 = ((bf16[32,2,1152]{2,1,0:T(2,128)(2,1)}), bf16[32,2,1152]{2,1,0:T(2,128)(2,1)S(1)}, u32[]{:S(2)}, u32[]{:S(2)}) async-start(bf16[32,2,1152]{2,1,0:T(2,128)(2,1)} %reshape.194), calls=%async_computation.2 | async-start | bytes 294912 | tf_op jit(solution)/shard_map/all_to_all | solution.py:32
  575.8 11.4 %all-to-all-start.3 = ((bf16[8,2,4608]{2,1,0:T(2,128)(2,1)}), bf16[8,2,4608]{2,1,0:T(2,128)(2,1)S(1)}, u32[]{:S(2)}, u32[]{:S(2)}) async-start(bf16[8,2,4608]{2,1,0:T(2,128)(2,1)} %reshape.196), calls=%async_computation.3 | async-start | bytes 294912 | tf_op jit(solution)/shard_map/all_to_all | solution.py:117
  595.3 31.3 %copy-start.10 = (bf16[128,128]{1,0:T(8,128)(2,1)S(1)}, bf16[128,128]{1,0:T(8,128)(2,1)}, u32[]{:S(2)}) copy-start(bf16[128,128]{1,0:T(8,128)(2,1)} %param.23) | copy-start | bytes 98308
Sparse Core Ops, SparseCore 0:
  520.9 40.6 all-gather.1
